TPU v7x, 32 devices: a whole 2x2x4 slice. The times are simulated.
32 devices in a mesh: dp: 16 (over z, y, core), expert: 2 (over x).
Axes of the slice: x: 2, y: 2, z: 4, core: 2. Of those that a mesh axis runs over, the one named last changes fastest.
Arguments:
- tokens: bfloat16 [256, 6144], P('dp', 'expert'), may hold values from -6 to 6
- expert_ids: int32 [256, 2], P('dp'), may hold values from 0 to 7, all different within a row; in each aligned block of 16 rows (0 to 15, 16 to 31, ...) at most 8 rows name the same one
- gate_probs: float32 [256, 2], P('dp'), may hold values from 0.1 to 1
- w_gate: bfloat16 [8, 6144, 8192], P('expert', None, 'dp'), may hold values from -0.078125 to 0.078125
- w_up: bfloat16 [8, 6144, 8192], P('expert', None, 'dp'), may hold values from -0.078125 to 0.078125
- w_down_t: bfloat16 [8, 6144, 8192], P('expert', 'dp'), may hold values from -0.0625 to 0.0625
Outputs:
- mixed: bfloat16 [256, 6144], P('dp', 'expert')
Inputs may be any that keep to these rules, and one draw needn't show every extreme that they name: `expert_ids`: each row names 2 different experts. Among the 16 rows of one index of dp no expert is named more than 8 times, a bound that some block reaches.
All inputs are finite; a program needn't handle non-finite values.
Results may differ from a plain program's by a relative error of at most 0.0057.
Values may be sent and summed in bfloat16 or wider, within the bound.
A program may use at most 128 MiB of HBM per device.

v0:
```python
import jax
import jax.numpy as jnp
from jax import lax
from jax.sharding import PartitionSpec as P


def assignments(expert_ids, experts, capacity):
    flat = expert_ids.reshape(-1)
    onehot = (flat[:, None] == jnp.arange(experts, dtype=jnp.int32)[None, :]).astype(jnp.int32)
    earlier = jnp.cumsum(onehot, axis=0) - onehot
    position = jnp.sum(earlier * onehot, axis=1).reshape(expert_ids.shape)
    expert_hit = (
        expert_ids[:, :, None] == jnp.arange(experts, dtype=jnp.int32)[None, None, :]
    ).astype(jnp.float32)
    slot_hit = (
        position[:, :, None] == jnp.arange(capacity, dtype=jnp.int32)[None, None, :]
    ).astype(jnp.float32)
    return (expert_hit, slot_hit)


def per_device(tokens, expert_ids, gate_probs, w_gate, w_up, w_down_t):
    local_experts = w_gate.shape[0]
    expert_count = lax.axis_size("expert")
    dp_count = lax.axis_size("dp")
    experts = local_experts * expert_count
    capacity = tokens.shape[0] // 2
    expert_hit, slot_hit = assignments(expert_ids, experts, capacity)
    dispatch_map = jnp.einsum("tke,tkc->ect", expert_hit, slot_hit).astype(jnp.bfloat16)
    combine_map = jnp.einsum(
        "tk,tke,tkc->tec", gate_probs, expert_hit, slot_hit, precision=lax.Precision.HIGHEST
    )
    slots = jnp.einsum(
        "ect,td->ecd", dispatch_map, tokens, preferred_element_type=jnp.float32
    ).astype(jnp.bfloat16)
    arrived = lax.all_to_all(slots, "expert", split_axis=0, concat_axis=2, tiled=True)
    piece = lax.all_gather(arrived, "dp", axis=1, tiled=True)
    gate = jnp.einsum("erd,edf->erf", piece, w_gate, preferred_element_type=jnp.float32)
    up = jnp.einsum("erd,edf->erf", piece, w_up, preferred_element_type=jnp.float32)
    hidden = (jax.nn.silu(gate) * up).astype(jnp.bfloat16)
    partial_out = jnp.einsum(
        "erf,edf->erd",
        lax.all_gather(hidden, "dp", axis=2, tiled=True),
        w_down_t,
        preferred_element_type=jnp.float32,
    )
    results = partial_out.astype(jnp.bfloat16).reshape(
        local_experts, dp_count, capacity, w_down_t.shape[1]
    )
    results = lax.all_to_all(results, "dp", split_axis=1, concat_axis=3, tiled=True)
    results = results.reshape(local_experts, capacity, results.shape[3])
    slice_width = tokens.shape[1]
    outgoing = results.reshape(local_experts, capacity, expert_count, slice_width)
    returned = lax.all_to_all(outgoing, "expert", split_axis=2, concat_axis=0, tiled=True)
    returned = returned.reshape(experts, capacity, slice_width)
    mixed = jnp.einsum(
        "tec,ecd->td", combine_map, returned.astype(jnp.float32), precision=lax.Precision.HIGHEST
    )
    return mixed.astype(jnp.bfloat16)


def solution(mesh):
    placed = (
        P("dp", "expert"),
        P("dp", None),
        P("dp", None),
        P("expert", None, "dp"),
        P("expert", None, "dp"),
        P("expert", "dp", None),
    )
    return jax.shard_map(
        per_device, mesh=mesh, in_specs=placed, out_specs=P("dp", "expert"), check_vma=False
    )
```

profile of v0, /device:TPU:0, one launch (start us, length us, event | category | flops | bytes accessed | tf_op | source)
XLA Modules:
  0.0 233.5 jit_solution(2106220213072693453)
XLA Ops:
  6.5 0.0 copy-start
  6.5 0.0 all-gather.3.cloned.1.call-start
  6.5 0.8 copy.17
  7.3 0.1 eq.46
  7.4 0.1 fusion.7
  7.5 0.1 reduce_window_sum.11
  7.5 0.2 select_reduce_fusion
  7.7 0.1 eq.50
  7.8 0.3 fusion.3
  8.1 0.1 copy.20
  8.2 0.0 copy-done
  8.2 0.2 convolution_convert_fusion
  8.5 10.6 %all_to_all.48 = bf16[8,8,3072]{2,1,0:T(8,128)(2,1)S(1)} all-to-all(bf16[8,8,3072]{2,1,0:T(8,128)(2,1)S(1)} %convolution_convert_fusion), channel_id=1, replica_groups=mesh['dp'=16,'expert'=2] {'expert'}, dimensions={0} | all-to-all | bytes 786432 | tf_op jit(solution)/shard_map/all_to_all | solution.py:35
  19.1 0.8 copy.21
  19.9 0.0 all-gather.3.cloned.1.call-update
  19.9 0.0 all-gather.5.cloned.1.call-start
  19.9 62.0 %all-gather.3.cloned.1.call-done = bf16[4,128,6144]{2,1,0:T(8,128)(2,1)} async-done(((bf16[4,8,6144]{2,1,0:T(8,128)(2,1)}), bf16[4,128,6144]{2,1,0:T(8,128)(2,1)}) %all-gather.3.cloned.1.call-update) | async-done | bytes 6291472 | tf_op jit(solution)/shard_map/all_gather | solution.py:36
  81.9 0.0 copy-start.2
  81.9 11.9 %fusion.16 = f32[4,128,512]{2,1,0:T(8,128)S(1)} fusion(bf16[4,128,6144]{2,1,0:T(8,128)(2,1)} %all-gather.3.cloned.1.call-done, bf16[4,6144,512]{2,1,0:T(8,128)(2,1)} %param.9), kind=kOutput, calls=%fused_computation.25 | convolution fusion | flops 3221225472 | bytes 32505856 | tf_op jit(solution)/shard_map/erd,edf->erf/dot_general | solution.py:37
  93.8 0.0 copy-done.2
  93.9 0.0 copy-start.1
  93.9 12.6 %fusion.1 = bf16[4,128,512]{2,1,0:T(8,128)(2,1)} fusion(bf16[4,128,6144]{2,1,0:T(8,128)(2,1)S(1)} %copy-done.2, bf16[4,6144,512]{2,1,0:T(8,128)(2,1)} %param.10, f32[4,128,512]{2,1,0:T(8,128)S(1)} %fusion.16), kind=kOutput, calls=%fused_computation.4 | convolution fusion | flops 3222798336 | bytes 33030144 | tf_op jit(solution)/shard_map/erd,edf->erf/dot_general | solution.py:38
  106.4 0.0 copy-start.3
  106.4 0.0 all-gather.5.cloned.1.call-update
  106.5 76.5 %all-gather.5.cloned.1.call-done = bf16[4,128,8192]{2,1,0:T(8,128)(2,1)} async-done(((bf16[4,128,512]{2,1,0:T(8,128)(2,1)}), bf16[4,128,8192]{2,1,0:T(8,128)(2,1)}) %all-gather.5.cloned.1.call-update) | async-done | bytes 8388624 | tf_op jit(solution)/shard_map/all_gather | solution.py:42
  183.0 14.5 %fusion.2 = bf16[4,16,8,384]{3,2,1,0:T(8,128)(2,1)S(1)} fusion(bf16[4,128,8192]{2,1,0:T(8,128)(2,1)} %all-gather.5.cloned.1.call-done, bf16[4,384,8192]{2,1,0:T(8,128)(2,1)} %param.11), kind=kOutput, calls=%fused_computation.6 | convolution fusion | flops 3221422080 | bytes 33947648 | tf_op jit(solution)/shard_map/erf,edf->erd/dot_general | solution.py:40
  197.5 0.8 copy.22
  198.3 3.6 %all-to-all-start.1 = ((bf16[4,16,8,384]{3,2,0,1:T(8,128)(2,1)}), bf16[4,16,8,384]{3,2,0,1:T(8,128)(2,1)S(1)}, u32[]{:S(2)}, u32[]{:S(2)}) async-start(bf16[4,16,8,384]{3,2,0,1:T(8,128)(2,1)} %copy.22), calls=%async_computation.1 | async-start | bytes 786432 | tf_op jit(solution)/shard_map/all_to_all | solution.py:49
  201.8 0.0 copy-done.3
  201.8 0.1 copy.18
  201.9 12.0 %all-to-all-done.1 = bf16[4,16,8,384]{3,2,0,1:T(8,128)(2,1)S(1)} async-done(((bf16[4,16,8,384]{3,2,0,1:T(8,128)(2,1)}), bf16[4,16,8,384]{3,2,0,1:T(8,128)(2,1)S(1)}, u32[]{:S(2)}, u32[]{:S(2)}) %all-to-all-start.1) | async-done | bytes 393248 | tf_op jit(solution)/shard_map/all_to_all | solution.py:49
  213.9 0.1 copy.23
  214.1 0.1 reshape_reshape.3
  214.2 0.8 copy.24
  215.0 3.5 %all-to-all-start.2 = ((bf16[4,8,2,3072]{3,1,0,2:T(8,128)(2,1)}), bf16[4,8,2,3072]{3,1,0,2:T(8,128)(2,1)S(1)}, u32[]{:S(2)}, u32[]{:S(2)}) async-start(bf16[4,8,2,3072]{3,1,0,2:T(8,128)(2,1)} %copy.24), calls=%async_computation.2 | async-start | bytes 786432 | tf_op jit(solution)/shard_map/all_to_all | solution.py:53
  218.5 0.4 fusion.6
  218.9 0.1 copy.26
  219.0 6.6 %all-to-all-done.2 = bf16[4,8,2,3072]{3,1,0,2:T(8,128)(2,1)S(1)} async-done(((bf16[4,8,2,3072]{3,1,0,2:T(8,128)(2,1)}), bf16[4,8,2,3072]{3,1,0,2:T(8,128)(2,1)S(1)}, u32[]{:S(2)}, u32[]{:S(2)}) %all-to-all-start.2) | async-done | bytes 393248 | tf_op jit(solution)/shard_map/all_to_all | solution.py:53
  225.6 1.1 fusion
  226.7 0.0 copy-done.1
Async XLA Ops:
  6.5 1.7 copy-start
  6.5 75.4 %all-gather.3.cloned.1.call-start = ((), (), s32[]{:S(2)}) async-start(), calls=%async_computation.3 | async-start | bytes 6684672 | tf_op jit(solution)/shard_map/all_gather | solution.py:36
  19.9 163.1 %all-gather.5.cloned.1.call-start = ((), (), s32[]{:S(2)}) async-start(), calls=%async_computation.4 | async-start | bytes 8912896 | tf_op jit(solution)/shard_map/all_gather | solution.py:42
  81.9 11.9 %copy-start.2 = (bf16[4,128,6144]{2,1,0:T(8,128)(2,1)S(1)}, bf16[4,128,6144]{2,1,0:T(8,128)(2,1)}, u32[]{:S(2)}) copy-start(bf16[4,128,6144]{2,1,0:T(8,128)(2,1)} %all-gather.3.cloned.1.call-done) | copy-start | bytes 18874372
  93.9 132.8 %copy-start.1 = (bf16[16,3072]{1,0:T(8,128)(2,1)S(1)}, bf16[16,3072]{1,0:T(8,128)(2,1)}, u32[]{:S(2)}) copy-start(bf16[16,3072]{1,0:T(8,128)(2,1)} %param.6) | copy-start | bytes 294916
  106.4 95.4 %copy-start.3 = (f32[16,2]{0,1:T(2,128)S(1)}, f32[16,2]{0,1:T(2,128)}, u32[]{:S(2)}) copy-start(f32[16,2]{0,1:T(2,128)} %param.8) | copy-start | bytes 388
  198.3 15.7 %all-to-all-start.1 = ((bf16[4,16,8,384]{3,2,0,1:T(8,128)(2,1)}), bf16[4,16,8,384]{3,2,0,1:T(8,128)(2,1)S(1)}, u32[]{:S(2)}, u32[]{:S(2)}) async-start(bf16[4,16,8,384]{3,2,0,1:T(8,128)(2,1)} %copy.22), calls=%async_computation.1 | async-start | bytes 786432 | tf_op jit(solution)/shard_map/all_to_all | solution.py:49
  215.0 10.6 %all-to-all-start.2 = ((bf16[4,8,2,3072]{3,1,0,2:T(8,128)(2,1)}), bf16[4,8,2,3072]{3,1,0,2:T(8,128)(2,1)S(1)}, u32[]{:S(2)}, u32[]{:S(2)}) async-start(bf16[4,8,2,3072]{3,1,0,2:T(8,128)(2,1)} %copy.24), calls=%async_computation.2 | async-start | bytes 786432 | tf_op jit(solution)/shard_map/all_to_all | solution.py:53
Sparse Core Ops, SparseCore 0:
  20.0 61.8 all-gather.2
  106.6 76.3 all-gather.4
where the time goes:
time: 234 us
  waiting for transfers between devices  157 us (67%)
  matrix products  41 us (18%)
  between operations  13.5 us (6%)
  blocking collectives  10.6 us (5%)
  starting transfers between devices  7.06 us (3%)
  local copies, waits for them, and re-layouts  3.83 us (2%)
    all_gather x1, waiting for transfers between devices, per_device(): lax.all_gather(hidden, 'dp', axis=2, tiled=True)  76.5 us
    all_gather x1, waiting for transfers between devices, per_device(): piece = lax.all_gather(arrived, 'dp', axis=1, tiled=True)  62 us
    dot_general x1, matrix products, per_device(): jnp.einsum('erf,edf->erd', lax.all_gather(hidden, 'dp', axis=2, tiled=Tru...  14.5 us
    dot_general x1, matrix products, per_device(): jnp.einsum('erd,edf->erf', piece, w_up, preferred_element_type=jnp.float32)  12.6 us
    all_to_all x1, waiting for transfers between devices, per_device(): lax.all_to_all(results, 'dp', split_axis=1, concat_axis=3, tiled=True)  12 us
    dot_general x1, matrix products, per_device(): jnp.einsum('erd,edf->erf', piece, w_gate, preferred_element_type=jnp.floa...  11.9 us
    all_to_all x1, blocking collectives, per_device(): lax.all_to_all(slots, 'expert', split_axis=0, concat_axis=2, tiled=True)  10.6 us
    all_to_all x1, waiting for transfers between devices, per_device(): lax.all_to_all(outgoing, 'expert', split_axis=2, concat_axis=0, tiled=True)  6.61 us
  transfers between devices with their start and end apart: 4, of which 4 were waited for; matrix products, arithmetic and copies ran while one was open for 0% of the time, Pallas kernels for 0%

commit v1 on v0

--- a/solution.py
+++ b/solution.py
@@ -1,6 +1,10 @@
+import functools
+
 import jax
 import jax.numpy as jnp
 from jax import lax
+from jax.experimental import pallas as pl
+from jax.experimental.pallas import tpu as pltpu
 from jax.sharding import PartitionSpec as P
 
 
@@ -18,7 +22,7 @@
     return (expert_hit, slot_hit)
 
 
-def per_device(tokens, expert_ids, gate_probs, w_gate, w_up, w_down_t):
+def gathered(tokens, expert_ids, gate_probs, w_gate, w_up, w_down_t):
     local_experts = w_gate.shape[0]
     expert_count = lax.axis_size("expert")
     dp_count = lax.axis_size("dp")
@@ -58,6 +62,296 @@
     return mixed.astype(jnp.bfloat16)
 
 
+MESH = pl.DeviceIdType.MESH
+META = 128
+
+
+def fused(
+    shape,
+    packed, w_gate, w_up, w_down, out,
+    tok, hid, xbuf, wg, wu, wd, acc, total, pbuf, fin,
+    x_send, x_recv, own_sem,
+    t_ring_send, t_ring_recv, t_part_send, t_part_recv,
+    h_ring_send, h_ring_recv, h_part_send, h_part_recv,
+    w_sem, d_sem, f_send, f_recv,
+):
+    experts, chips, block, capacity, half = shape
+    dp, x = lax.axis_index("dp"), lax.axis_index("expert")
+    chip, core = dp // 2, dp % 2
+    odd = chip % 2
+    place = (1 - odd) * (chip // 2) + odd * (chips - 1 - chip // 2)
+
+    def chip_at(position):
+        p = (position + chips) % chips
+        back = p // (chips // 2)
+        return (1 - back) * (2 * p) + back * (2 * (chips - 1 - p) + 1)
+
+    right = (chip_at(place + 1) * 2 + core, x)
+    left = (chip_at(place - 1) * 2 + core, x)
+    partner = (chip * 2 + 1 - core, x)
+    opposite = (dp, 1 - x)
+
+    def send(src, dst, send_sem, recv_sem, device):
+        pltpu.make_async_remote_copy(
+            src_ref=src, dst_ref=dst, send_sem=send_sem, recv_sem=recv_sem,
+            device_id=device, device_id_type=MESH,
+        ).start()
+
+    def wait(ref, sem):
+        pltpu.make_async_copy(ref, ref, sem).wait()
+
+    def hops(q, way):
+        longer = chips // 2
+        return longer if q % 2 == way else chips - 1 - longer
+
+    def ring(buffer, index, ring_send, ring_recv, part_send, part_recv):
+        def own(q, src):
+            dst = buffer.at[index(q), core, chip]
+            send(src, dst, ring_send.at[q], ring_recv.at[q, 0, 0], right)
+            send(src, dst, ring_send.at[q], ring_recv.at[q, 1, 0], left)
+            send(src, dst, part_send.at[q], part_recv.at[q], partner)
+
+        def serve(q, hop):
+            for way in range(2):
+                count = hops(q, way)
+                if hop > count:
+                    continue
+                origin = chip_at(place - hop if way == 0 else place + hop)
+                arrived = buffer.at[index(q), core, origin]
+                wait(arrived, ring_recv.at[q, way, hop - 1])
+                if hop < count:
+                    send(
+                        arrived, arrived, ring_send.at[q], ring_recv.at[q, way, hop],
+                        right if way == 0 else left,
+                    )
+                send(arrived, arrived, part_send.at[q], part_recv.at[q], partner)
+
+        def others(q):
+            wait(buffer.at[index(q), 1 - core], part_recv.at[q])
+
+        def sent(q):
+            wait(buffer.at[index(q), core, pl.ds(0, chips - 1)], ring_send.at[q])
+            wait(buffer.at[index(q), core], part_send.at[q])
+
+        return own, serve, others, sent
+
+    def load_up(e):
+        s = e % 2
+        pltpu.make_async_copy(w_gate.at[e], wg.at[s], w_sem.at[0, s]).start()
+        pltpu.make_async_copy(w_up.at[e], wu.at[s], w_sem.at[1, s]).start()
+
+    def load_down(e):
+        pltpu.make_async_copy(w_down.at[e], wd.at[e % 2], d_sem.at[e % 2]).start()
+
+    longest = chips // 2
+
+    own, serve, others, sent = ring(
+        tok, lambda q: x if q == 0 else 1 - x,
+        t_ring_send, t_ring_recv, t_part_send, t_part_recv,
+    )
+    send(packed, tok.at[x, core, chip], x_send, x_recv, opposite)
+    own(0, packed)
+    pltpu.make_async_copy(packed, tok.at[x, core, chip], own_sem).start()
+    for e in range(min(2, experts)):
+        load_up(e)
+    wait(tok.at[1 - x, core, chip], x_recv)
+    own(1, tok.at[1 - x, core, chip])
+    for hop in range(1, longest + 1):
+        serve(0, hop)
+        serve(1, hop)
+    wait(packed, x_send)
+    pltpu.make_async_copy(packed, tok.at[x, core, chip], own_sem).wait()
+    for q in range(2):
+        others(q)
+        sent(q)
+
+    blocks = 2 * chips
+    tokens, rows = blocks * block, blocks * capacity
+    meta = tok[0, :, :, :, half:half + META].reshape(tokens, META).astype(jnp.float32)
+    token_of = lax.broadcasted_iota(jnp.int32, (tokens, rows), 0)
+    slot_of = lax.broadcasted_iota(jnp.int32, (tokens, rows), 1)
+    same_block = (token_of // block) == (slot_of // capacity)
+    slot_in = slot_of % capacity
+
+    def weights(e):
+        key = ((x * experts + e) * capacity + slot_in).astype(jnp.float32)
+        hit = [jnp.where(same_block & (meta[:, k:k + 1] == key), 1.0, 0.0) for k in range(2)]
+        prob = [meta[:, 2 + k:3 + k] + meta[:, 4 + k:5 + k] + meta[:, 6 + k:7 + k] for k in range(2)]
+        return hit[0] + hit[1], hit[0] * prob[0] + hit[1] * prob[1]
+
+    tile = half // 3 if half % 384 == 0 else half
+    per_half = half // tile
+    units = wg.shape[2]
+    width = 256 if units % 256 == 0 else units
+
+    def compute_up(e):
+        s = e % 2
+        chosen = weights(e)[0].astype(jnp.bfloat16)
+
+        @pl.loop(0, 2 * per_half)
+        def _(k):
+            first = pl.multiple_of((k % per_half) * tile, 128)
+            piece = tok[k // per_half, :, :, :, pl.ds(first, tile)].reshape(tokens, tile)
+            picked = lax.dot_general(
+                chosen, piece, (((0,), (0,)), ((), ())), preferred_element_type=jnp.float32
+            )
+            xbuf[:, pl.ds(pl.multiple_of(k * tile, 128), tile)] = picked.astype(jnp.bfloat16)
+
+        wait(wg.at[s], w_sem.at[0, s])
+        wait(wu.at[s], w_sem.at[1, s])
+
+        @pl.loop(0, units // width)
+        def _(n):
+            columns = pl.ds(pl.multiple_of(n * width, 128), width)
+            gate = jnp.dot(xbuf[...], wg[s, :, columns], preferred_element_type=jnp.float32)
+            up = jnp.dot(xbuf[...], wu[s, :, columns], preferred_element_type=jnp.float32)
+            hidden = gate / (1.0 + jnp.exp(-gate)) * up
+            hid[e, core, chip, :, columns] = hidden.astype(jnp.bfloat16)
+
+    def compute_down(e):
+        s = e % 2
+        wait(wd.at[s], d_sem.at[s])
+        acc[...] = jnp.zeros_like(acc)
+
+        @pl.loop(0, blocks)
+        def _(b):
+            first = ((b % chips) * 2 + b // chips) * units
+            acc[...] += lax.dot_general(
+                hid[e, b // chips, b % chips],
+                wd[s, :, pl.ds(pl.multiple_of(first, 128), units)],
+                (((1,), (1,)), ((), ())), preferred_element_type=jnp.float32,
+            )
+
+        result = acc[...].astype(jnp.bfloat16)
+        weight = weights(e)[1]
+        high = weight.astype(jnp.bfloat16)
+        low = (weight - high.astype(jnp.float32)).astype(jnp.bfloat16)
+        term = jnp.dot(high, result, preferred_element_type=jnp.float32)
+        term = term + jnp.dot(low, result, preferred_element_type=jnp.float32)
+        if e == 0:
+            total[...] = term
+        else:
+            total[...] += term
+
+    own, serve, others, sent = ring(
+        hid, lambda e: e, h_ring_send, h_ring_recv, h_part_send, h_part_recv
+    )
+    for stage in range(experts + longest):
+        if stage < experts:
+            compute_up(stage)
+            own(stage, hid.at[stage, core, chip])
+            if stage + 2 < experts:
+                load_up(stage + 2)
+            if stage == experts - 1:
+                for e in range(min(2, experts)):
+                    load_down(e)
+        for e in range(experts):
+            if 1 <= stage - e <= longest:
+                serve(e, stage - e)
+        e = stage - longest
+        if e >= 0:
+            others(e)
+            compute_down(e)
+            if e + 2 < experts:
+                load_down(e + 2)
+
+    pbuf[...] = total[...].astype(jnp.bfloat16).reshape(pbuf.shape)
+    side, lane = dp // chips, dp % chips
+    slot = lane * 2 + x
+    here = side == x
+    for step in range(1, blocks):
+        j = (dp + step) % blocks
+        send(pbuf.at[j % 2, j // 2], fin.at[slot], f_send.at[step], f_recv.at[slot], (j, side))
+
+    mine = pbuf.at[core, chip]
+
+    @pl.when(here)
+    def _():
+        pltpu.make_async_copy(mine, fin.at[slot], f_send.at[0]).start()
+        pltpu.make_async_copy(mine, fin.at[slot], f_send.at[0]).wait()
+
+    @pl.when(jnp.logical_not(here))
+    def _():
+        send(mine, fin.at[slot], f_send.at[0], f_recv.at[slot], (dp, side))
+        wait(mine, f_send.at[0])
+
+    for e in range(experts):
+        sent(e)
+    for source in range(blocks):
+        from_here = here & (slot == source)
+
+        @pl.when(jnp.logical_not(from_here))
+        def _():
+            wait(fin.at[source], f_recv.at[source])
+
+    features = fin.shape[2]
+    for i in range(chips):
+        both = fin[2 * i].astype(jnp.float32) + fin[2 * i + 1].astype(jnp.float32)
+        out[:, i * features:(i + 1) * features] = both.astype(jnp.bfloat16)
+    for step in range(1, blocks):
+        j = (dp + step) % blocks
+        wait(pbuf.at[j % 2, j // 2], f_send.at[step])
+
+
+def per_device(tokens, expert_ids, gate_probs, w_gate, w_up, w_down_t):
+    experts, depth, units = w_gate.shape
+    block, half = tokens.shape
+    features, wide = w_down_t.shape[1:]
+    dp_count, expert_count = lax.axis_size("dp"), lax.axis_size("expert")
+    capacity = block // 2
+    chips = dp_count // 2
+    fits = (
+        expert_count == 2 and chips >= 4 and chips % 2 == 0 and block == 16
+        and half % 128 == 0 and units % 128 == 0 and features % 128 == 0
+        and chips * capacity * 2 % 128 == 0 and 8 * experts * depth * units <= 2 ** 27
+    )
+    if not fits:
+        return gathered(tokens, expert_ids, gate_probs, w_gate, w_up, w_down_t)
+    flat = expert_ids.reshape(-1)
+    same = (flat[:, None] == flat[None, :]) & (
+        jnp.arange(2 * block)[:, None] > jnp.arange(2 * block)[None, :]
+    )
+    position = jnp.sum(same.astype(jnp.int32), axis=1).reshape(expert_ids.shape)
+    slots = (expert_ids * capacity + position).astype(jnp.float32)
+    high = lax.reduce_precision(gate_probs, 8, 7)
+    middle = lax.reduce_precision(gate_probs - high, 8, 7)
+    low = gate_probs - high - middle
+    meta = jnp.concatenate([slots, high, middle, low], axis=1).astype(jnp.bfloat16)
+    meta = jnp.pad(meta, ((0, 0), (0, META - meta.shape[1])))
+    packed = jnp.concatenate([tokens, meta], axis=1)
+
+    longest = chips // 2
+    rows = dp_count * capacity
+    bf, dma = jnp.bfloat16, pltpu.SemaphoreType.DMA
+    vmem, anywhere = pl.BlockSpec(memory_space=pltpu.VMEM), pl.BlockSpec(memory_space=pl.ANY)
+    return pl.pallas_call(
+        functools.partial(fused, (experts, chips, block, capacity, half)),
+        out_shape=jax.ShapeDtypeStruct((block, half), bf),
+        in_specs=[vmem, anywhere, anywhere, anywhere],
+        out_specs=vmem,
+        scratch_shapes=[
+            pltpu.VMEM((2, 2, chips, block, half + META), bf),
+            pltpu.VMEM((experts, 2, chips, rows, units), bf),
+            pltpu.VMEM((rows, depth), bf),
+            pltpu.VMEM((2, depth, units), bf),
+            pltpu.VMEM((2, depth, units), bf),
+            pltpu.VMEM((2, features, wide), bf),
+            pltpu.VMEM((rows, features), jnp.float32),
+            pltpu.VMEM((dp_count * block, features), jnp.float32),
+            pltpu.VMEM((2, chips, block, features), bf),
+            pltpu.VMEM((dp_count, block, features), bf),
+            dma, dma, dma,
+            dma((2,)), dma((2, 2, longest)), dma((2,)), dma((2,)),
+            dma((experts,)), dma((experts, 2, longest)), dma((experts,)), dma((experts,)),
+            dma((2, 2)), dma((2,)), dma((dp_count,)), dma((dp_count,)),
+        ],
+        compiler_params=pltpu.CompilerParams(
+            has_side_effects=True, vmem_limit_bytes=62 * 2 ** 20
+        ),
+        name="fused_experts",
+    )(packed, w_gate, w_up, w_down_t)
+
+
 def solution(mesh):
     placed = (
         P("dp", "expert"),

time: 234 us -> 106 us (0.45)
  waiting for transfers between devices: 157 us -> 0 us
  Pallas kernels: 0 us -> 98.7 us
  matrix products: 41 us -> 0 us
  between operations: 13.5 us -> 0.03 us
  blocking collectives: 10.6 us -> 0 us
  starting transfers between devices: 7.06 us -> 0 us
  other arithmetic: 0.31 us -> 3.19 us
    all_gather x2 -> x0, waiting for transfers between devices: 139 us -> none  [the longest x1 76.5 us: per_device(): lax.all_gather(hidden, 'dp', axis=2, tiled=True)]
    pallas_call x0 -> x1, Pallas kernels: none -> 98.7 us  [per_device(): pl.pallas_call(functools.partial(fused, (experts, chips, block, capacity,...]
    dot_general x7 -> x0, matrix products: 41 us -> none  [the longest x1 14.5 us: per_device(): jnp.einsum('erf,edf->erd', lax.all_gather(hidden, 'dp', axis=2, tiled=Tru...]
    all_to_all x2 -> x0, waiting for transfers between devices: 18.6 us -> none  [the longest x1 12 us: per_device(): lax.all_to_all(results, 'dp', split_axis=1, concat_axis=3, tiled=True)]
    all_to_all x1 -> x0, blocking collectives: 10.6 us -> none  [per_device(): lax.all_to_all(slots, 'expert', split_axis=0, concat_axis=2, tiled=True)]
    all_to_all x2 -> x0, starting transfers between devices: 7.02 us -> none  [the longest x1 3.55 us: per_device(): lax.all_to_all(results, 'dp', split_axis=1, concat_axis=3, tiled=True)]
  transfers between devices with their start and end apart: 4 -> 0, of which waited for: 4 -> 0; matrix products, arithmetic and copies ran while one was open for 0% -> 0% of each run, Pallas kernels for 0% -> 0%
where the time goes in v1:
time: 106 us; the launch traced here: 105 us
  Pallas kernels  98.7 us (93%)
  local copies, waits for them, and re-layouts  3.39 us (3%)
  other arithmetic  3.19 us (3%)
    pallas_call x1, Pallas kernels, per_device(): pl.pallas_call(functools.partial(fused, (experts, chips, block, capacity,...  98.7 us
    unnamed x3, local copies, waits for them, and re-layouts  3.06 us

profile of v1, /device:TPU:0, one launch (start us, length us, event | category | flops | bytes accessed | tf_op | source)
XLA Modules:
  0.0 105.3 jit_solution(9926443471073836345)
XLA Ops:
  0.0 0.7 broadcast_multiply_fusion
  0.7 0.7 reduce_precision.6
  1.4 0.1 copy.24
  1.4 0.1 copy.23
  1.5 0.8 copy.22
  2.3 0.1 eq.15
  2.4 0.2 convert_reduce_fusion
  2.6 0.1 reshape.5
  2.7 0.8 copy.25
  3.4 0.1 fusion.8
  3.5 1.5 %pad_maximum_fusion.packed = bf16[16,3200]{1,0:T(8,128)(2,1)} fusion(bf16[16,128]{1,0:T(8,128)(2,1)S(1)} %fusion.8, bf16[16,3072]{1,0:T(8,128)(2,1)} %param.6), kind=kLoop, calls=%fused_computation | loop fusion | flops 204800 | bytes 204800 | tf_op jit(solution)/shard_map/concatenate | solution.py:321
  5.1 98.7 %fused_experts.1 = bf16[16,3072]{1,0:T(8,128)(2,1)} custom-call(bf16[16,3200]{1,0:T(8,128)(2,1)} %pad_maximum_fusion.packed, bf16[4,6144,512]{2,1,0:T(8,128)(2,1)} %w_gate.1, bf16[4,6144,512]{2,1,0:T(8,128)(2,1)} %w_up.1, bf16[4,384,8192]{2,1,0:T(8,128)(2,1)} %w_down.1), custom_call_target="tpu_custom_call" | custom-call | tf_op jit(solution)/shard_map/fused_experts/pallas_call | solution.py:327
  103.8 1.5 %copy.28 = bf16[16,3072]{1,0:T(8,128)(2,1)} copy(bf16[16,3072]{1,0:T(8,128)(2,1)} %fused_experts.1) | data formatting | bytes 196608
  (2 shorter events, 0.0 us)

commit v2 on v1

--- a/solution.py
+++ b/solution.py
@@ -188,7 +188,7 @@
         s = e % 2
         chosen = weights(e)[0].astype(jnp.bfloat16)
 
-        @pl.loop(0, 2 * per_half)
+        @pl.loop(0, 2 * per_half, unroll=2)
         def _(k):
             first = pl.multiple_of((k % per_half) * tile, 128)
             piece = tok[k // per_half, :, :, :, pl.ds(first, tile)].reshape(tokens, tile)
@@ -213,7 +213,7 @@
         wait(wd.at[s], d_sem.at[s])
         acc[...] = jnp.zeros_like(acc)
 
-        @pl.loop(0, blocks)
+        @pl.loop(0, blocks, unroll=4)
         def _(b):
             first = ((b % chips) * 2 + b // chips) * units
             acc[...] += lax.dot_general(

time: 106 us -> 99.6 us (0.940)
  Pallas kernels: 98.7 us -> 92.2 us
    pallas_call x1, Pallas kernels: 98.7 us -> 92.2 us  [per_device(): pl.pallas_call(functools.partial(fused, (experts, chips, block, capacity,...]
where the time goes in v2:
time: 99.6 us; the launch traced here: 98.8 us
  Pallas kernels  92.2 us (93%)
  local copies, waits for them, and re-layouts  3.39 us (3%)
  other arithmetic  3.19 us (3%)
    pallas_call x1, Pallas kernels, per_device(): pl.pallas_call(functools.partial(fused, (experts, chips, block, capacity,...  92.2 us
    unnamed x3, local copies, waits for them, and re-layouts  3.06 us

profile of v2, /device:TPU:0, one launch (start us, length us, event | category | flops | bytes accessed | tf_op | source)
XLA Modules:
  0.0 98.8 jit_solution(204151749799239849)
XLA Ops:
  0.0 0.7 broadcast_multiply_fusion
  0.7 0.7 reduce_precision.6
  1.4 0.1 copy.24
  1.4 0.1 copy.23
  1.5 0.8 copy.22
  2.3 0.1 eq.15
  2.4 0.2 convert_reduce_fusion
  2.6 0.1 reshape.5
  2.7 0.8 copy.25
  3.4 0.1 fusion.8
  3.5 1.5 %pad_maximum_fusion.packed = bf16[16,3200]{1,0:T(8,128)(2,1)} fusion(bf16[16,128]{1,0:T(8,128)(2,1)S(1)} %fusion.8, bf16[16,3072]{1,0:T(8,128)(2,1)} %param.6), kind=kLoop, calls=%fused_computation | loop fusion | flops 204800 | bytes 204800 | tf_op jit(solution)/shard_map/concatenate | solution.py:321
  5.1 92.2 %fused_experts.1 = bf16[16,3072]{1,0:T(8,128)(2,1)} custom-call(bf16[16,3200]{1,0:T(8,128)(2,1)} %pad_maximum_fusion.packed, bf16[4,6144,512]{2,1,0:T(8,128)(2,1)} %w_gate.1, bf16[4,6144,512]{2,1,0:T(8,128)(2,1)} %w_up.1, bf16[4,384,8192]{2,1,0:T(8,128)(2,1)} %w_down.1), custom_call_target="tpu_custom_call" | custom-call | tf_op jit(solution)/shard_map/fused_experts/pallas_call | solution.py:327
  97.3 1.5 %copy.28 = bf16[16,3072]{1,0:T(8,128)(2,1)} copy(bf16[16,3072]{1,0:T(8,128)(2,1)} %fused_experts.1) | data formatting | bytes 196608
  (2 shorter events, 0.0 us)
